TPU v7x, 128 devices: a whole 4x4x4 slice. The times are simulated.
128 devices in a mesh: row: 32 (over z, x, y_lo), col: 4 (over y_hi, core).
Axes of the slice: x: 4, y: 4 (y_hi: 2, y_lo: 2; y = y_hi * 2 + y_lo), z: 4, core: 2. Of those that a mesh axis runs over, the one named last changes fastest.
Arguments:
- trailing: float32 [65536, 8192], P('row', 'col'), may hold values from -6 to 6
- vectors: float32 [65536, 256], P(('row', 'col')), may hold values from -0.09375 to 0.09375
- tfactor: float32 [256, 256], replicated, may hold values from -0.375 to 0.375
Outputs:
- updated: float32 [65536, 8192], P('row', 'col')
All inputs are finite; a program needn't handle non-finite values.
Results may differ from a plain program's by a relative error of at most 0.0003.
Values sent between devices are 32-bit elements.
A program may use at most 128 MiB of HBM per device.

v0:
```python
import functools

import jax
import jax.numpy as jnp
from jax import lax
from jax.experimental import pallas as pl
from jax.experimental.pallas import tpu as pltpu
from jax.sharding import PartitionSpec as P

MESH = pl.DeviceIdType.MESH
F32, BF16 = jnp.float32, jnp.bfloat16
HALVES = 2
PIECES = 4
QUARTERS = 2
G_QUARTERS = 8
LAG = 2


def split(x):
    high = x.astype(BF16)
    return high, (x - high.astype(F32)).astype(BF16)


def dot3(a_high, a_low, b_high, b_low):
    dot = functools.partial(jnp.dot, preferred_element_type=F32)
    return dot(a_high, b_high) + (dot(a_low, b_high) + dot(a_high, b_low))


def sum_kernel(
    ring, c_hbm, v_hbm, t_hbm, c_ref, near, scaled,
    acc, vt, got, t_ref, c_sem, l_sem,
    sib_send, sib_recv, y_send, y_recv, f_send, f_recv, r_send, r_recv, g_send, g_recv,
):
    row, col = lax.axis_index("row"), lax.axis_index("col")
    core, y = lax.rem(col, 2), lax.div(col, 2)
    sibling = y * 2 + (1 - core)
    across = (1 - y) * 2 + core
    across_sibling = (1 - y) * 2 + (1 - core)
    half = ring // 2
    z, x = lax.div(row, 2), lax.rem(row, 2)
    at = jnp.where(x == 0, z, ring - 1 - z)

    def row_of(place):
        return jnp.where(place < half, 2 * place, 2 * (ring - 1 - place) + 1)

    def wrap(i):
        return lax.rem(i + 2 * ring, ring)

    hops = (row_of(wrap(at + 1)), row_of(wrap(at - 1)))
    blocks, own, depth = near.shape
    width = c_ref.shape[2]
    part_depth = depth // HALVES
    steps = ring - 1

    def chunk_of(i):
        step = lax.div(i, 2) + 1
        return jnp.where(i == ring - 1, at, wrap(jnp.where(lax.rem(i, 2) == 0, at - step, at + step)))

    def c_copy(chunk):
        return pltpu.make_async_copy(
            c_hbm.at[:, pl.ds(pl.multiple_of(chunk * width, width), width)], c_ref.at[chunk], c_sem.at[chunk]
        )

    v_copy = pltpu.make_async_copy(v_hbm, near.at[col], l_sem.at[0])
    t_copy = pltpu.make_async_copy(t_hbm, t_ref, l_sem.at[1])
    v_copy.start()

    barrier = pltpu.get_barrier_semaphore()
    friends = [(row, sibling), (row, across), (hops[0], col), (hops[1], col)]
    for friend in friends:
        pl.semaphore_signal(barrier, inc=1, device_id=friend, device_id_type=MESH)
    pl.semaphore_wait(barrier, len(friends))

    def remote(src, dst, send, recv, to):
        return pltpu.make_async_remote_copy(
            src_ref=src, dst_ref=dst, send_sem=send, recv_sem=recv, device_id=to, device_id_type=MESH
        )

    size = own // PIECES

    def y_copy(h, q):
        there = (pl.ds(q * size, size), pl.ds(h * part_depth, part_depth))
        return remote(near.at[(col,) + there], near.at[(col,) + there], y_send.at[h, q], y_recv.at[h, q], (row, across))

    def forward(h, q):
        there = (across, pl.ds(q * size, size), pl.ds(h * part_depth, part_depth))
        return remote(near.at[there], near.at[there], f_send.at[h, q], f_recv.at[h, q], (row, sibling))

    v_copy.wait()
    for h in range(HALVES):
        for q in range(PIECES):
            y_copy(h, q).start()
    sib = remote(near.at[col], near.at[col], sib_send, sib_recv, (row, sibling))
    sib.start()

    def load(i, carry):
        c_copy(chunk_of(i)).start()
        return carry

    lax.fori_loop(0, ring, load, 0)
    t_copy.start()

    def keep(block, h):
        high, low = split(near[block, :, h * part_depth:(h + 1) * part_depth].T)
        vt[h, block, :part_depth] = high
        vt[h, block, part_depth:] = low

    for h in range(HALVES):
        keep(col, h)
    sib.wait()
    for h in range(HALVES):
        keep(sibling, h)

    def arrive(h):
        for q in range(PIECES):
            y_copy(h, q).wait()
            forward(h, q).start()
        keep(across, h)
        for q in range(PIECES):
            forward(h, q).wait()
        keep(across_sibling, h)

    def product(h, block, high, low):
        both = jnp.dot(vt[h, block], high, preferred_element_type=F32)
        return both[:part_depth] + (
            both[part_depth:] + jnp.dot(vt[h, block, :part_depth], low, preferred_element_type=F32)
        )

    def pieces_of(chunk, pair):
        return [(b, split(c_ref[chunk, pl.ds(pl.multiple_of(b * own, own), own)])) for b in pair]

    def near_job(i, carry):
        chunk = chunk_of(i)
        c_copy(chunk).wait()
        (b0, c0), (b1, c1) = pieces_of(chunk, (col, sibling))
        for h in range(HALVES):
            acc[chunk, h * part_depth:(h + 1) * part_depth] = product(h, b0, *c0) + product(h, b1, *c1)
        return carry

    def job(i, h):
        chunk = chunk_of(i)
        (b0, c0), (b1, c1) = pieces_of(chunk, (across, across_sibling))
        acc[chunk, h * part_depth:(h + 1) * part_depth] += product(h, b0, *c0) + product(h, b1, *c1)

    def first_job(i, carry):
        job(i, 0)
        return carry

    def later_job(i, carry):
        job(i, 1)
        return carry

    part = part_depth // (2 * QUARTERS)

    def sum_send(h, way, step, q, src):
        rows = pl.ds(((h * 2 + way) * QUARTERS + q) * part, part)
        lane = h * 2 + way
        return remote(
            src.at[rows], got.at[step, rows], r_send.at[lane, step, q], r_recv.at[lane, step, q], (hops[way], col)
        )

    def begin(h):
        for q in range(QUARTERS):
            for way in range(2):
                sum_send(h, way, 0, q, acc.at[chunk_of(way)]).start()

    def reduce(h, step):
        for q in range(QUARTERS):
            for way in range(2):
                rows = pl.ds(((h * 2 + way) * QUARTERS + q) * part, part)
                chunk = wrap(at - 2 - step) if way == 0 else wrap(at + 2 + step)
                sum_send(h, way, step, q, got.at[step]).wait_recv()
                got[step, rows] += acc[chunk, rows]

                @pl.when(step < steps - 1)
                def _():
                    sum_send(h, way, step + 1, q, got.at[step]).start()

    lax.fori_loop(0, ring, near_job, 0)
    arrive(0)
    lax.fori_loop(0, 2, first_job, 0)
    begin(0)
    lax.fori_loop(2, ring, first_job, 0)

    def early(t, carry):
        reduce(0, t)
        return carry

    def both_halves(t, carry):
        reduce(0, t)

        @pl.when(t >= LAG)
        def _():
            reduce(1, t - LAG)

        jobs = 2 * (t - LAG + 2)
        lax.fori_loop(jnp.minimum(jobs, ring), jnp.minimum(jobs + 2, ring), later_job, 0)
        return carry

    def late(t, carry):
        reduce(1, t - LAG)
        return carry

    lax.fori_loop(0, LAG - 1, early, 0)
    arrive(1)
    lax.fori_loop(0, 2, later_job, 0)
    begin(1)
    lax.fori_loop(LAG - 1, steps, both_halves, 0)
    t_copy.wait()
    t_high, t_low = split(t_ref[...])
    lax.fori_loop(steps, steps + LAG, late, 0)

    high, low = split(got[steps - 1])
    scaled[at] = dot3(t_high, t_low, high, low)
    g_part = depth // (2 * G_QUARTERS)

    def gather_send(way, step, q, chunk):
        ref = scaled.at[chunk, pl.ds((way * G_QUARTERS + q) * g_part, g_part)]
        return remote(ref, ref, g_send.at[way, step, q], g_recv.at[way, step, q], (hops[way], col))

    for q in range(G_QUARTERS):
        for way in range(2):
            gather_send(way, 0, q, at).start()

    def gather(step, carry):
        for q in range(G_QUARTERS):
            for way in range(2):
                chunk = wrap(at - 1 - step) if way == 0 else wrap(at + 1 + step)
                gather_send(way, step, q, chunk).wait_recv()

                @pl.when(step < steps - 1)
                def _():
                    gather_send(way, step + 1, q, chunk).start()

        return carry

    lax.fori_loop(0, steps, gather, 0)

    def sent(step, carry):
        for way in range(2):
            for h in range(HALVES):
                for q in range(QUARTERS):
                    sum_send(h, way, step, q, got.at[step]).wait_send()
            for q in range(G_QUARTERS):
                gather_send(way, step, q, at).wait_send()
        return carry

    lax.fori_loop(0, steps, sent, 0)


def update_kernel(c_ref, near, scaled, out_hbm, v_high, v_low, stage, sem):
    ring, height, width = c_ref.shape
    blocks, own, _ = near.shape
    for b in range(blocks):
        v_high[pl.ds(b * own, own)], v_low[pl.ds(b * own, own)] = split(near[b])
    slots = stage.shape[0]

    def out_copy(chunk, slot):
        return pltpu.make_async_copy(
            stage.at[slot], out_hbm.at[:, pl.ds(pl.multiple_of(chunk * width, width), width)], sem.at[slot]
        )

    def step(chunk, carry):
        slot = lax.rem(chunk, slots)

        @pl.when(chunk >= slots)
        def _():
            out_copy(chunk - slots, slot).wait()

        high, low = split(scaled[chunk])
        for b in range(blocks):
            rows = pl.ds(b * own, own)
            stage[slot, rows] = c_ref[chunk, rows] - dot3(v_high[rows], v_low[rows], high, low)
        out_copy(chunk, slot).start()
        return carry

    lax.fori_loop(0, ring, step, 0)
    for i in range(slots):
        chunk = ring - slots + i
        out_copy(chunk, chunk % slots).wait()


def ring_shards(ring, trailing, vectors, tfactor):
    height, columns = trailing.shape
    own, depth = vectors.shape
    width = columns // ring
    blocks = height // own
    steps = ring - 1
    dma = pltpu.SemaphoreType.DMA
    vmem = pl.BlockSpec(memory_space=pltpu.VMEM)
    hbm = pl.BlockSpec(memory_space=pl.ANY)
    held, near, scaled = pl.pallas_call(
        functools.partial(sum_kernel, ring),
        out_shape=(
            pltpu.VMEM((ring, height, width), F32),
            pltpu.VMEM((blocks, own, depth), F32),
            pltpu.VMEM((ring, depth, width), F32),
        ),
        in_specs=[hbm, hbm, hbm],
        out_specs=(vmem, vmem, vmem),
        scratch_shapes=[
            pltpu.VMEM((ring, depth, width), F32),
            pltpu.VMEM((HALVES, blocks, 2 * depth // HALVES, own), BF16),
            pltpu.VMEM((steps, depth, width), F32),
            pltpu.VMEM((depth, depth), F32),
            dma((ring,)), dma((2,)),
            dma, dma,
            dma((HALVES, PIECES)), dma((HALVES, PIECES)), dma((HALVES, PIECES)), dma((HALVES, PIECES)),
            dma((2 * HALVES, steps, QUARTERS)), dma((2 * HALVES, steps, QUARTERS)),
            dma((2, steps, G_QUARTERS)), dma((2, steps, G_QUARTERS)),
        ],
        compiler_params=pltpu.CompilerParams(
            collective_id=0, has_side_effects=True, vmem_limit_bytes=20 << 20
        ),
    )(trailing, vectors, tfactor)
    slots = min(4, ring)
    return pl.pallas_call(
        update_kernel,
        out_shape=jax.ShapeDtypeStruct((height, columns), F32),
        in_specs=[vmem, vmem, vmem],
        out_specs=hbm,
        scratch_shapes=[
            pltpu.VMEM((height, depth), BF16),
            pltpu.VMEM((height, depth), BF16),
            pltpu.VMEM((slots, height, width), F32),
            dma((slots,)),
        ],
        compiler_params=pltpu.CompilerParams(vmem_limit_bytes=20 << 20),
    )(held, near, scaled)


def plain_shards(trailing, vectors, tfactor):
    dot = functools.partial(jnp.dot, precision=lax.Precision.HIGH, preferred_element_type=F32)
    near_vectors = lax.all_gather(vectors, "col", axis=0, tiled=True)
    summed = lax.psum(dot(near_vectors.T, trailing), "row")
    return trailing - dot(near_vectors, dot(tfactor, summed))


def solution(mesh):
    ring, columns = mesh.shape["row"], mesh.shape["col"]
    placed = (P("row", "col"), P(("row", "col"), None), P())

    def shards(trailing, vectors, tfactor):
        width = trailing.shape[1] // ring
        if columns == 4 and ring % 2 == 0 and ring > 2 * LAG and width % 128 == 0:
            return ring_shards(ring, trailing, vectors, tfactor)
        return plain_shards(trailing, vectors, tfactor)

    return jax.shard_map(
        shards, mesh=mesh, in_specs=placed, out_specs=P("row", "col"), check_vma=False
    )
```

profile of v0, /device:TPU:0, one launch (start us, length us, event | category | flops | bytes accessed | tf_op | source)
XLA Modules:
  0.0 405.2 jit_solution(11748247743418708062)
XLA Ops:
  6.5 0.0 copy-start
  6.5 0.0 all-gather.2.cloned.1.call-start
  6.5 0.7 all-gather.2.cloned.1.call-update
  7.3 0.0 all-reduce.2.cloned.1.call-start
  7.3 31.0 %all-gather.2.cloned.1.call-done = f32[2048,256]{1,0:T(8,128)} async-done(((f32[512,256]{1,0:T(8,128)}), f32[2048,256]{1,0:T(8,128)}) %all-gather.2.cloned.1.call-update) | async-done | bytes 2097168 | tf_op jit(solution)/shard_map/all_gather | solution.py:334
  38.3 12.3 %fusion = f32[256,2048]{1,0:T(8,128)} fusion(f32[2048,256]{1,0:T(8,128)} %all-gather.2.cloned.1.call-done, f32[2048,2048]{1,0:T(8,128)} %param.3), kind=kOutput, calls=%fused_computation.1 | convolution fusion | flops 6442450944 | bytes 20971520 | tf_op jit(solution)/shard_map/dot_general | solution.py:335
  50.6 0.0 all-reduce.2.cloned.1.call-update
  50.7 17.6 %copy.4 = f32[2048,2048]{0,1:T(8,128)} copy(f32[2048,2048]{1,0:T(8,128)} %param.3) | data formatting | bytes 33554432 | tf_op args[0]
  68.3 0.0 copy-start.2
  68.3 295.3 %all-reduce.2.cloned.1.call-done = f32[256,2048]{1,0:T(8,128)} async-done(((f32[256,2048]{1,0:T(8,128)}), f32[256,2048]{1,0:T(8,128)}) %all-reduce.2.cloned.1.call-update) | async-done | bytes 2097168 | tf_op jit(solution)/shard_map/psum | solution.py:335
  363.6 0.0 copy-done
  363.6 3.4 fusion.1
  367.0 0.0 copy-done.2
  367.0 13.7 %bitcast_subtract_fusion = f32[2048,2048]{0,1:T(8,128)} fusion(f32[2048,2048]{0,1:T(8,128)} %copy.4, f32[2048,256]{1,0:T(8,128)S(1)} %fusion.1, f32[2048,256]{1,0:T(8,128)S(1)} %copy-done.2), kind=kOutput, calls=%fused_computation | convolution fusion | flops 6446645248 | bytes 37748736 | tf_op jit(solution)/shard_map/dot_general | solution.py:336
  380.7 0.0 copy-start.1
  380.7 17.6 %copy.5 = f32[2048,2048]{1,0:T(8,128)} copy(f32[2048,2048]{0,1:T(8,128)} %bitcast_subtract_fusion) | data formatting | bytes 33554432 | tf_op jit(solution)/shard_map/sub | solution.py:336
  398.3 0.0 copy-done.1
Async XLA Ops:
  6.5 357.0 %copy-start = (f32[256,256]{1,0:T(8,128)S(1)}, f32[256,256]{1,0:T(8,128)}, u32[]{:S(2)}) copy-start(f32[256,256]{1,0:T(8,128)} %param.5) | copy-start | bytes 786436
  6.5 31.8 %all-gather.2.cloned.1.call-start = ((), (), s32[]{:S(2)}) async-start(), calls=%async_computation | async-start | bytes 2621440 | tf_op jit(solution)/shard_map/all_gather | solution.py:334
  7.3 356.3 %all-reduce.2.cloned.1.call-start = ((), (), s32[]{:S(2)}) async-start(), calls=%async_computation.1 | async-start | bytes 4194304 | tf_op jit(solution)/shard_map/psum | solution.py:335
  68.3 298.7 %copy-start.2 = (f32[2048,256]{1,0:T(8,128)S(1)}, f32[2048,256]{1,0:T(8,128)}, u32[]{:S(2)}) copy-start(f32[2048,256]{1,0:T(8,128)} %all-gather.2.cloned.1.call-done) | copy-start | bytes 6291460
  380.7 17.6 %copy-start.1 = (f32[256,256]{1,0:T(8,128)S(1)}, f32[256,256]{1,0:T(8,128)}, u32[]{:S(2)}) copy-start(f32[256,256]{1,0:T(8,128)} %param.5) | copy-start | bytes 786436
Sparse Core Ops, SparseCore 0:
  9.0 29.2 all-gather.1
  50.8 312.7 all-reduce.1
where the time goes:
time: 406 us; the launch traced here: 405 us
  waiting for transfers between devices  327 us (81%)
  local copies, waits for them, and re-layouts  35.3 us (9%)
  matrix products  29.4 us (7%)
  between operations  13.4 us (3%)
    psum x1, waiting for transfers between devices, plain_shards(): summed = lax.psum(dot(near_vectors.T, trailing), 'row')  295 us
    all_gather x1, waiting for transfers between devices, plain_shards(): near_vectors = lax.all_gather(vectors, 'col', axis=0, tiled=True)  31 us
    sub x1, local copies, waits for them, and re-layouts, plain_shards(): return trailing - dot(near_vectors, dot(tfactor, summed))  17.6 us
    unnamed x7, local copies, waits for them, and re-layouts  17.6 us
    dot_general x2, matrix products, plain_shards(): return trailing - dot(near_vectors, dot(tfactor, summed))  17.1 us
    dot_general x1, matrix products, plain_shards(): summed = lax.psum(dot(near_vectors.T, trailing), 'row')  12.3 us
  transfers between devices with their start and end apart: 2, of which 2 were waited for; matrix products, arithmetic and copies ran while one was open for 4% of the time, Pallas kernels for 0%

commit v1 on v0

v1 whole, which is shorter than its diff:
```python
import functools

import jax
import jax.numpy as jnp
from jax import lax
from jax.experimental import pallas as pl
from jax.experimental.pallas import tpu as pltpu
from jax.sharding import PartitionSpec as P

MESH = pl.DeviceIdType.MESH
F32, BF16 = jnp.float32, jnp.bfloat16
RING = 4
HALVES = 2
V_PIECES = 2
AWAY = (2, 1, 3)
OTHERS = ((0, 1), (1, 0), (3, 0), (1, 1), (3, 1), (2, 0), (2, 1))


def split(x):
    high = x.astype(BF16)
    return high, (x - high.astype(F32)).astype(BF16)


def dot(a, b):
    return jnp.dot(a, b, preferred_element_type=F32)


def dot3(a_high, a_low, b_high, b_low):
    return dot(a_high, b_high) + (dot(a_low, b_high) + dot(a_high, b_low))


def sum_kernel(
    c_hbm, v_hbm, t_hbm, c_ref, w_high, w_low, res,
    near, acc, vt, got1, got2, t_ref, c_sem, l_sem,
    sib_send, sib_recv, v_send, v_recv, f_send, f_recv,
    r1_send, r1_recv, r2_send, r2_recv, g2_send, g2_recv, g1_send, g1_recv,
):
    row, col = lax.axis_index("row"), lax.axis_index("col")
    core, y_hi = lax.rem(col, 2), lax.div(col, 2)
    z, x, y_lo = lax.div(row, 2 * RING), lax.rem(lax.div(row, 2), RING), lax.rem(row, 2)
    sibling = y_hi * 2 + (1 - core)
    across = (1 - y_hi) * 2 + core
    across_sibling = (1 - y_hi) * 2 + (1 - core)
    blocks, own, depth = near.shape
    chunks, height, width = c_ref.shape
    part = depth // HALVES
    sub = part // (2 * RING)
    pos, other = (x, z), (z, x)

    def wrap(i):
        return lax.rem(i + RING, RING)

    def target(d, away, across_other, flip):
        first = wrap(pos[d] + away)
        second = wrap(other[d] + across_other)
        zz, xx = (second, first) if d == 0 else (first, second)
        return (zz * (2 * RING) + xx * 2 + lax.rem(y_lo + flip, 2), col)

    def remote(src, dst, send, recv, to):
        return pltpu.make_async_remote_copy(
            src_ref=src, dst_ref=dst, send_sem=send, recv_sem=recv, device_id=to, device_id_type=MESH
        )

    def chunk_of(d, away):
        return d * RING + wrap(pos[d] + away)

    order = [(d, away) for away in AWAY + (0,) for d in range(2)]

    def c_copy(chunk):
        return pltpu.make_async_copy(
            c_hbm.at[:, pl.ds(pl.multiple_of(chunk * width, width), width)], c_ref.at[chunk], c_sem.at[chunk]
        )

    v_copy = pltpu.make_async_copy(v_hbm, near.at[col], l_sem.at[0])
    t_copy = pltpu.make_async_copy(t_hbm, t_ref, l_sem.at[1])
    v_copy.start()
    t_copy.start()
    for d, away in order:
        c_copy(chunk_of(d, away)).start()

    barrier = pltpu.get_barrier_semaphore()
    friends = [(row, sibling), (row, across)]
    friends += [target(d, away, 0, 0) for d in range(2) for away in AWAY]
    friends += [target(0, 0, q, 1) for q in range(RING)]
    friends += [target(1, 0, q, 1) for q in range(1, RING)]
    for friend in friends:
        pl.semaphore_signal(barrier, inc=1, device_id=friend, device_id_type=MESH)
    pl.semaphore_wait(barrier, len(friends))

    size = own // V_PIECES

    def v_copy_across(h, p):
        there = near.at[col, pl.ds(p * size, size), pl.ds(h * part, part)]
        return remote(there, there, v_send.at[h, p], v_recv.at[h, p], (row, across))

    def forward(h, p):
        there = near.at[across, pl.ds(p * size, size), pl.ds(h * part, part)]
        return remote(there, there, f_send.at[h, p], f_recv.at[h, p], (row, sibling))

    v_copy.wait()
    for h in range(HALVES):
        for p in range(V_PIECES):
            v_copy_across(h, p).start()
    sib = remote(near.at[col], near.at[col], sib_send, sib_recv, (row, sibling))
    sib.start()

    def keep(block, h):
        high, low = split(near[block, :, h * part:(h + 1) * part].T)
        vt[h, block, :part] = high
        vt[h, block, part:] = low

    def arrive(h):
        for p in range(V_PIECES):
            v_copy_across(h, p).wait()
            forward(h, p).start()
        keep(across, h)
        for p in range(V_PIECES):
            forward(h, p).wait()
        keep(across_sibling, h)

    def product(h, block, high, low):
        both = dot(vt[h, block], high)
        return both[:part] + (both[part:] + dot(vt[h, block, :part], low))

    def pieces_of(chunk, pair):
        return [(b, split(c_ref[chunk, pl.ds(pl.multiple_of(b * own, own), own)])) for b in pair]

    def near_job(chunk):
        (b0, c0), (b1, c1) = pieces_of(chunk, (col, sibling))
        for h in range(HALVES):
            acc[h, chunk] = product(h, b0, *c0) + product(h, b1, *c1)

    def job(chunk, h):
        (b0, c0), (b1, c1) = pieces_of(chunk, (across, across_sibling))
        acc[h, chunk] += product(h, b0, *c0) + product(h, b1, *c1)

    def weigh(block, t_high, t_low):
        high, low = split(near[block])
        rows = pl.ds(pl.multiple_of(block * own, own), own)
        w_high[rows], w_low[rows] = split(dot3(high, low, t_high, t_low))

    def r1_copy(h, d, i):
        chunk = chunk_of(d, AWAY[i])
        return remote(
            acc.at[h, chunk], got1.at[h, d, i], r1_send.at[h, d, i], r1_recv.at[h, d, i], target(d, AWAY[i], 0, 0)
        )

    def rows_of(d, e):
        q, flip = (0, 0) if e == 0 else OTHERS[e - 1]
        return wrap(other[d] - q) * 2 + lax.rem(y_lo + flip, 2)

    def r2_copy(h, d, e):
        q, flip = OTHERS[e - 1]
        place = wrap(other[d] + q) * 2 + lax.rem(y_lo + flip, 2)
        rows = pl.ds(pl.multiple_of(place * sub, sub), sub)
        return remote(
            acc.at[h, chunk_of(d, 0), rows], got2.at[h, d, e], r2_send.at[h, d, e], r2_recv.at[h, d, e],
            target(d, 0, q, flip),
        )

    def res_rows(h, d, e):
        return pl.ds(pl.multiple_of(h * part + rows_of(d, e) * sub, sub), sub)

    def g2_copy(h, d, e):
        q, flip = OTHERS[e - 1]
        ref = res.at[chunk_of(d, 0), res_rows(h, d, 0)]
        return remote(ref, ref, g2_send.at[h, d, e], g2_recv.at[h, d, e], target(d, 0, q, flip))

    def g1_copy(h, d, i, e):
        ref = res.at[chunk_of(d, 0), res_rows(h, d, e)]
        return remote(ref, ref, g1_send.at[h, d, i, e], g1_recv.at[h, d, i, e], target(d, AWAY[i], 0, 0))

    def produce(h):
        for d, away in order:
            job(chunk_of(d, away), h)
            if away:
                r1_copy(h, d, AWAY.index(away)).start()

    def collect(h):
        for d in range(2):
            mine = chunk_of(d, 0)
            for i in range(3):
                r1_copy(h, d, i).wait_recv()
            acc[h, mine] += got1[h, d, 0] + (got1[h, d, 1] + got1[h, d, 2])
            for e in range(1, 2 * RING):
                r2_copy(h, d, e).start()

    def finish(h):
        for d in range(2):
            mine = chunk_of(d, 0)
            for e in range(1, 2 * RING):
                r2_copy(h, d, e).wait_recv()
            total = acc[h, mine, pl.ds(pl.multiple_of(rows_of(d, 0) * sub, sub), sub)]
            for e in range(1, 2 * RING):
                total += got2[h, d, e]
            res[mine, res_rows(h, d, 0)] = total
            for e in range(1, 2 * RING):
                g2_copy(h, d, e).start()
            for i in range(3):
                g1_copy(h, d, i, 0).start()

    def spread(h):
        for e in range(1, 2 * RING):
            for d in range(2):
                g2_copy(h, d, e).wait_recv()
                for i in range(3):
                    g1_copy(h, d, i, e).start()

    def gathered(h):
        for e in range(2 * RING):
            for d in range(2):
                for i in range(3):
                    g1_copy(h, d, i, e).wait_recv()

    for h in range(HALVES):
        keep(col, h)
    t_copy.wait()
    sib.wait()
    for h in range(HALVES):
        keep(sibling, h)
    for d, away in order:
        chunk = chunk_of(d, away)
        c_copy(chunk).wait()
        near_job(chunk)
    t_high, t_low = split(t_ref[...])
    weigh(col, t_high, t_low)
    arrive(0)
    produce(0)
    weigh(sibling, t_high, t_low)
    arrive(1)
    produce(1)
    collect(0)
    weigh(across, t_high, t_low)
    finish(0)
    weigh(across_sibling, t_high, t_low)
    collect(1)
    spread(0)
    finish(1)
    spread(1)
    gathered(0)
    gathered(1)

    for h in range(HALVES):
        for d in range(2):
            for i in range(3):
                r1_copy(h, d, i).wait_send()
                for e in range(2 * RING):
                    g1_copy(h, d, i, e).wait_send()
            for e in range(1, 2 * RING):
                r2_copy(h, d, e).wait_send()
                g2_copy(h, d, e).wait_send()


def update_kernel(c_ref, w_high, w_low, res, out_hbm, stage, sem):
    chunks, height, width = c_ref.shape
    slots = stage.shape[0]
    own = height // 4

    def out_copy(chunk, slot):
        return pltpu.make_async_copy(
            stage.at[slot], out_hbm.at[:, pl.ds(pl.multiple_of(chunk * width, width), width)], sem.at[slot]
        )

    def step(chunk, carry):
        slot = lax.rem(chunk, slots)

        @pl.when(chunk >= slots)
        def _():
            out_copy(chunk - slots, slot).wait()

        high, low = split(res[chunk])
        for b in range(4):
            rows = pl.ds(b * own, own)
            stage[slot, rows] = c_ref[chunk, rows] - dot3(w_high[rows], w_low[rows], high, low)
        out_copy(chunk, slot).start()
        return carry

    lax.fori_loop(0, chunks, step, 0)
    for i in range(slots):
        chunk = chunks - slots + i
        out_copy(chunk, chunk % slots).wait()


def grid_shards(trailing, vectors, tfactor):
    height, columns = trailing.shape
    own, depth = vectors.shape
    chunks = 2 * RING
    width = columns // chunks
    blocks = height // own
    part = depth // HALVES
    sub = part // (2 * RING)
    dma = pltpu.SemaphoreType.DMA
    vmem = pl.BlockSpec(memory_space=pltpu.VMEM)
    hbm = pl.BlockSpec(memory_space=pl.ANY)
    held, w_high, w_low, res = pl.pallas_call(
        sum_kernel,
        out_shape=(
            pltpu.VMEM((chunks, height, width), F32),
            pltpu.VMEM((height, depth), BF16),
            pltpu.VMEM((height, depth), BF16),
            pltpu.VMEM((chunks, depth, width), F32),
        ),
        in_specs=[hbm, hbm, hbm],
        out_specs=(vmem, vmem, vmem, vmem),
        scratch_shapes=[
            pltpu.VMEM((blocks, own, depth), F32),
            pltpu.VMEM((HALVES, chunks, part, width), F32),
            pltpu.VMEM((HALVES, blocks, 2 * part, own), BF16),
            pltpu.VMEM((HALVES, 2, 3, part, width), F32),
            pltpu.VMEM((HALVES, 2, 2 * RING, sub, width), F32),
            pltpu.VMEM((depth, depth), F32),
            dma((chunks,)), dma((2,)),
            dma, dma,
            dma((HALVES, V_PIECES)), dma((HALVES, V_PIECES)), dma((HALVES, V_PIECES)), dma((HALVES, V_PIECES)),
            dma((HALVES, 2, 3)), dma((HALVES, 2, 3)),
            dma((HALVES, 2, 2 * RING)), dma((HALVES, 2, 2 * RING)),
            dma((HALVES, 2, 2 * RING)), dma((HALVES, 2, 2 * RING)),
            dma((HALVES, 2, 3, 2 * RING)), dma((HALVES, 2, 3, 2 * RING)),
        ],
        compiler_params=pltpu.CompilerParams(
            collective_id=0, has_side_effects=True, vmem_limit_bytes=20 << 20
        ),
    )(trailing, vectors, tfactor)
    slots = 4
    return pl.pallas_call(
        update_kernel,
        out_shape=jax.ShapeDtypeStruct((height, columns), F32),
        in_specs=[vmem, vmem, vmem, vmem],
        out_specs=hbm,
        scratch_shapes=[pltpu.VMEM((slots, height, width), F32), dma((slots,))],
        compiler_params=pltpu.CompilerParams(vmem_limit_bytes=20 << 20),
    )(held, w_high, w_low, res)


def plain_shards(trailing, vectors, tfactor):
    dot = functools.partial(jnp.dot, precision=lax.Precision.HIGH, preferred_element_type=F32)
    near_vectors = lax.all_gather(vectors, "col", axis=0, tiled=True)
    summed = lax.psum(dot(near_vectors.T, trailing), "row")
    return trailing - dot(near_vectors, dot(tfactor, summed))


def solution(mesh):
    placed = (P("row", "col"), P(("row", "col"), None), P())
    fits = mesh.shape["row"] == 2 * RING * RING and mesh.shape["col"] == 4

    def shards(trailing, vectors, tfactor):
        if fits and trailing.shape == (2048, 2048) and vectors.shape == (512, 256):
            return grid_shards(trailing, vectors, tfactor)
        return plain_shards(trailing, vectors, tfactor)

    return jax.shard_map(
        shards, mesh=mesh, in_specs=placed, out_specs=P("row", "col"), check_vma=False
    )
```

time: 406 us -> 68.5 us (0.17)
  waiting for transfers between devices: 327 us -> 0 us
  Pallas kernels: 0 us -> 66.3 us
  local copies, waits for them, and re-layouts: 35.3 us -> 1.99 us
  matrix products: 29.4 us -> 0 us
  between operations: 13.4 us -> 0.01 us
    psum x1 -> x0, waiting for transfers between devices: 295 us -> none  [plain_shards(): summed = lax.psum(dot(near_vectors.T, trailing), 'row')]
    pallas_call x0 -> x2, Pallas kernels: none -> 66.3 us  [the longest x1 57 us: grid_shards(): pl.pallas_call(sum_kernel, out_shape=(pltpu.VMEM((chunks, height, width),...]
    all_gather x1 -> x0, waiting for transfers between devices: 31 us -> none  [plain_shards(): near_vectors = lax.all_gather(vectors, 'col', axis=0, tiled=True)]
    dot_general x3 -> x0, matrix products: 29.4 us -> none  [the longest x2 17.1 us: plain_shards(): return trailing - dot(near_vectors, dot(tfactor, summed))]
    sub x1 -> x0, local copies, waits for them, and re-layouts: 17.6 us -> none  [plain_shards(): return trailing - dot(near_vectors, dot(tfactor, summed))]
    unnamed x7 -> x4, local copies, waits for them, and re-layouts: 17.6 us -> 1.99 us
  transfers between devices with their start and end apart: 2 -> 0, of which waited for: 2 -> 0; matrix products, arithmetic and copies ran while one was open for 4% -> 0% of each run, Pallas kernels for 0% -> 0%
where the time goes in v1:
time: 68.5 us; the launch traced here: 68.3 us
  Pallas kernels  66.3 us (97%)
  local copies, waits for them, and re-layouts  1.99 us (3%)
    pallas_call x1, Pallas kernels, grid_shards(): pl.pallas_call(sum_kernel, out_shape=(pltpu.VMEM((chunks, height, width),...  57 us
    pallas_call x1, Pallas kernels, grid_shards(): pl.pallas_call(update_kernel, out_shape=jax.ShapeDtypeStruct((height, col...  9.25 us
    unnamed x4, local copies, waits for them, and re-layouts  1.99 us

profile of v1, /device:TPU:0, one launch (start us, length us, event | category | flops | bytes accessed | tf_op | source)
XLA Modules:
  0.0 68.3 jit_solution(8710530479110264712)
XLA Ops:
  0.0 0.0 copy-start
  0.0 1.0 %copy-done = f32[512,256]{1,0:T(8,128)S(1)} copy-done((f32[512,256]{1,0:T(8,128)S(1)}, f32[512,256]{1,0:T(8,128)}, u32[]{:S(2)}) %copy-start) | copy-done | bytes 524312
  1.0 0.0 copy-start.1
  1.0 0.9 %copy-done.1 = f32[256,256]{1,0:T(8,128)S(1)} copy-done((f32[256,256]{1,0:T(8,128)S(1)}, f32[256,256]{1,0:T(8,128)}, u32[]{:S(2)}) %copy-start.1) | copy-done | bytes 262168
  2.0 57.0 %shard_map.37 = (f32[8,2048,256]{2,1,0:T(8,128)S(1)}, bf16[2048,256]{1,0:T(8,128)(2,1)S(1)}, bf16[2048,256]{1,0:T(8,128)(2,1)S(1)}, f32[8,256,256]{2,1,0:T(8,128)S(1)}) custom-call(f32[2048,2048]{1,0:T(8,128)} %c_hbm.1, f32[512,256]{1,0:T(8,128)S(1)} %copy-done, f32[256,256]{1,0:T(8,128)S(1)} %copy-done.1), custom_call_target="tpu_custom_call" | custom-call | tf_op jit(solution)/shard_map/pallas_call | solution.py:295
  59.0 9.3 %shard_map.38 = f32[2048,2048]{1,0:T(8,128)} custom-call(f32[8,2048,256]{2,1,0:T(8,128)S(1)} %get-tuple-element.9.c_ref, bf16[2048,256]{1,0:T(8,128)(2,1)S(1)} %get-tuple-element.10.w_high, bf16[2048,256]{1,0:T(8,128)(2,1)S(1)} %get-tuple-element.11.w_low, f32[8,256,256]{2,1,0:T(8,128)S(1)} %get-tuple-element.12.res), custom_call_target="tpu_custom_call" | custom-call | tf_op jit(solution)/shard_map/pallas_call | solution.py:325
Async XLA Ops:
  0.0 1.0 %copy-start = (f32[512,256]{1,0:T(8,128)S(1)}, f32[512,256]{1,0:T(8,128)}, u32[]{:S(2)}) copy-start(f32[512,256]{1,0:T(8,128)} %v_hbm.1) | copy-start | bytes 1572868
  1.0 0.9 %copy-start.1 = (f32[256,256]{1,0:T(8,128)S(1)}, f32[256,256]{1,0:T(8,128)}, u32[]{:S(2)}) copy-start(f32[256,256]{1,0:T(8,128)} %t_hbm.1) | copy-start | bytes 786436

commit v2 on v1

v2 whole, which is shorter than its diff:
```python
import functools

import jax
import jax.numpy as jnp
from jax import lax
from jax.experimental import pallas as pl
from jax.experimental.pallas import tpu as pltpu
from jax.sharding import PartitionSpec as P

MESH = pl.DeviceIdType.MESH
F32, BF16 = jnp.float32, jnp.bfloat16
RING = 4
HALVES = 2
V_PIECES = 2
WAYS = (1, -1)
OTHERS = (0, 1, -1, 2)


def split(x):
    high = x.astype(BF16)
    return high, (x - high.astype(F32)).astype(BF16)


def dot(a, b):
    return jnp.dot(a, b, preferred_element_type=F32)


def dot3(a_high, a_low, b_high, b_low):
    return dot(a_high, b_high) + (dot(a_low, b_high) + dot(a_high, b_low))


def stacked(x):
    high, low = split(x)
    return jnp.concatenate([high, high, low], axis=0)


def sum_kernel(
    c_hbm, v_hbm, t_hbm, c_ref, w_ref, res,
    near, acc, vt, passing, got1, got2, got3, t_ref, c_sem, l_sem,
    send, sib_recv, v_recv, f_recv, a_recv, r1_recv, r2_recv, y_recv, g2_recv, g1_recv, near_recv, far_recv,
):
    row, col = lax.axis_index("row"), lax.axis_index("col")
    core, y_hi = lax.rem(col, 2), lax.div(col, 2)
    z, x, y_lo = lax.div(row, 2 * RING), lax.rem(lax.div(row, 2), RING), lax.rem(row, 2)
    sibling = y_hi * 2 + (1 - core)
    across = (1 - y_hi) * 2 + core
    across_sibling = (1 - y_hi) * 2 + (1 - core)
    blocks, own, depth = near.shape
    chunks, height, width = c_ref.shape
    part = depth // HALVES
    sub = part // RING
    half = part // 2
    group = range(1, RING)
    dims = range(2)
    pos, other = (x, z), (z, x)

    def wrap(i):
        return lax.rem(i + RING, RING)

    def target(d, away, across_other, flip):
        first = wrap(pos[d] + away)
        second = wrap(other[d] + across_other)
        zz, xx = (second, first) if d == 0 else (first, second)
        return (zz * (2 * RING) + xx * 2 + lax.rem(y_lo + flip, 2), col)

    def remote(src, dst, recv, to):
        return pltpu.make_async_remote_copy(
            src_ref=src, dst_ref=dst, send_sem=send, recv_sem=recv, device_id=to, device_id_type=MESH
        )

    def take(ref, sem):
        pltpu.make_async_copy(ref, ref, sem).wait()

    def chunk_of(d, away):
        return d * RING + wrap(pos[d] + away)

    order = [(d, away) for away in (2, 1, -1, 0) for d in dims]

    def c_copy(i):
        chunk = chunk_of(*order[i])
        return pltpu.make_async_copy(
            c_hbm.at[:, pl.ds(pl.multiple_of(chunk * width, width), width)], c_ref.at[chunk], c_sem.at[i]
        )

    v_copy = pltpu.make_async_copy(v_hbm, near.at[col], l_sem.at[0])
    t_copy = pltpu.make_async_copy(t_hbm, t_ref, l_sem.at[1])
    v_copy.start()
    t_copy.start()

    barrier = pltpu.get_barrier_semaphore()
    friends = [(row, sibling), (row, across)]
    friends += [target(d, away, 0, 0) for d in dims for away in (1, -1, 2)]
    friends += [target(0, 0, 0, 1)]
    for friend in friends:
        pl.semaphore_signal(barrier, inc=1, device_id=friend, device_id_type=MESH)
    v_copy.wait()
    t_copy.wait()
    for i in range(chunks):
        c_copy(i).start()
    pl.semaphore_wait(barrier, len(friends))

    size = own // V_PIECES

    def v_copy_across(h, p):
        there = near.at[col, pl.ds(p * size, size), pl.ds(h * part, part)]
        return remote(there, there, v_recv.at[h, p], (row, across))

    def forward(h, p):
        there = near.at[across, pl.ds(p * size, size), pl.ds(h * part, part)]
        return remote(there, there, f_recv.at[h], (row, sibling))

    for h in range(HALVES):
        for p in range(V_PIECES):
            v_copy_across(h, p).start()
    sib = remote(near.at[col], near.at[col], sib_recv, (row, sibling))
    sib.start()

    def keep(block, h):
        high, low = split(near[block, :, h * part:(h + 1) * part].T)
        vt[h, block, :part] = high
        vt[h, block, part:] = low

    def arrive(h):
        for p in range(V_PIECES):
            v_copy_across(h, p).wait_recv()
            forward(h, p).start()
        keep(across, h)

    def arrive_sibling(h):
        take(near.at[across_sibling, :, pl.ds(h * part, part)], f_recv.at[h])
        keep(across_sibling, h)

    def product(h, block, high, low):
        both = dot(vt[h, block], high)
        return both[:part] + (both[part:] + dot(vt[h, block, :part], low))

    def pieces_of(chunk, pair):
        return [(b, split(c_ref[chunk, pl.ds(pl.multiple_of(b * own, own), own)])) for b in pair]

    def near_job(chunk):
        (b0, c0), (b1, c1) = pieces_of(chunk, (col, sibling))
        for h in range(HALVES):
            acc[h, chunk] = product(h, b0, *c0) + product(h, b1, *c1)

    def job(chunk, h):
        (b0, c0), (b1, c1) = pieces_of(chunk, (across, across_sibling))
        acc[h, chunk] += product(h, b0, *c0) + product(h, b1, *c1)

    def weigh(block):
        t_high, t_low = split(t_ref[...])
        high, low = split(near[block])
        high, low = split(dot3(high, low, t_high, t_low))
        rows = pl.ds(pl.multiple_of(block * own, own), own)
        for h in range(HALVES):
            lanes = slice(h * part, (h + 1) * part)
            first = 3 * h * part
            w_ref[rows, first:first + part] = high[:, lanes]
            w_ref[rows, first + part:first + 2 * part] = low[:, lanes]
            w_ref[rows, first + 2 * part:first + 3 * part] = high[:, lanes]

    def upper(way):
        return slice(0, half) if way == 0 else slice(half, part)

    def lower(way):
        return slice(half, part) if way == 0 else slice(0, half)

    def a_copy(h, d, way):
        return remote(
            acc.at[h, chunk_of(d, 2), upper(way)], passing.at[h, d, way],
            a_recv.at[h, d, way], target(d, WAYS[way], 0, 0),
        )

    def b_copy(h, d, way):
        return remote(
            acc.at[h, chunk_of(d, WAYS[way]), lower(way)], got1.at[h, d, way, lower(way)],
            r1_recv.at[h, d], target(d, WAYS[way], 0, 0),
        )

    def s_copy(h, d, way):
        return remote(
            acc.at[h, chunk_of(d, WAYS[way]), upper(way)], got1.at[h, d, way, upper(way)],
            r1_recv.at[h, d], target(d, WAYS[way], 0, 0),
        )

    def place_rows(d, away):
        return pl.ds(pl.multiple_of(wrap(other[d] + away) * sub, sub), sub)

    def r2_copy(h, d, e):
        return remote(
            acc.at[h, chunk_of(d, 0), place_rows(d, OTHERS[e])], got2.at[h, d, e - 1], r2_recv.at[h, d],
            target(d, 0, OTHERS[e], 0),
        )

    def y_copy(h, d):
        return remote(
            acc.at[h, chunk_of(d, 0), place_rows(d, 0)], got3.at[h, d], y_recv.at[h, d], target(d, 0, 0, 1)
        )

    def res_rows(h, d, e):
        return pl.ds(pl.multiple_of(h * part + wrap(other[d] - OTHERS[e]) * sub, sub), sub)

    def g2_copy(h, d, e):
        ref = res.at[chunk_of(d, 0), res_rows(h, d, 0)]
        return remote(ref, ref, g2_recv.at[h, d, e], target(d, 0, OTHERS[e], 0))

    def g1_copy(h, d, way, e):
        ref = res.at[chunk_of(d, 0), res_rows(h, d, e)]
        recv = g1_recv.at[h, d, e] if way == e % 2 else near_recv.at[h]
        return remote(ref, ref, recv, target(d, WAYS[way], 0, 0))

    def gf_copy(h, d, e):
        way = e % 2
        ref = res.at[chunk_of(d, -WAYS[way]), res_rows(h, d, e)]
        return remote(ref, ref, far_recv.at[h], target(d, WAYS[way], 0, 0))

    def produce(h):
        for d in dims:
            job(chunk_of(d, 2), h)
        for d in dims:
            for way in range(2):
                a_copy(h, d, way).start()
        for way in range(2):
            for d in dims:
                job(chunk_of(d, WAYS[way]), h)
            for d in dims:
                b_copy(h, d, way).start()
        for d in dims:
            job(chunk_of(d, 0), h)

    def pass_on(h):
        for d in dims:
            for way in range(2):
                a_copy(h, d, way).wait_recv()
                acc[h, chunk_of(d, WAYS[way]), upper(way)] += passing[h, d, way]
                s_copy(h, d, way).start()

    def collect(h):
        for d in dims:
            mine = chunk_of(d, 0)
            take(got1.at[h, d], r1_recv.at[h, d])
            acc[h, mine] += got1[h, d, 0] + got1[h, d, 1]
            for e in group:
                r2_copy(h, d, e).start()

    def pair(h):
        for d in dims:
            take(got2.at[h, d], r2_recv.at[h, d])
            acc[h, chunk_of(d, 0), place_rows(d, 0)] += got2[h, d, 0] + (got2[h, d, 1] + got2[h, d, 2])
            y_copy(h, d).start()

    def finish(h):
        for d in dims:
            mine = chunk_of(d, 0)
            y_copy(h, d).wait_recv()
            res[mine, res_rows(h, d, 0)] = acc[h, mine, place_rows(d, 0)] + got3[h, d]
            for e in group:
                g2_copy(h, d, e).start()
            for way in range(2):
                g1_copy(h, d, way, 0).start()

    def spread(h, e):
        for d in dims:
            g2_copy(h, d, e).wait_recv()
            for way in range(2):
                g1_copy(h, d, way, e).start()

    def hand_on(h, e):
        for d in dims:
            g1_copy(h, d, e % 2, e).wait_recv()
            gf_copy(h, d, e).start()

    def near_gathered(h):
        take(res.at[0], near_recv.at[h])

    def far_gathered(h):
        take(res.at[0], far_recv.at[h])

    def update(chunk):
        right = stacked(res[chunk, :part])
        for b in range(blocks):
            rows = slice(b * own, (b + 1) * own)
            c_ref[chunk, rows] = c_ref[chunk, rows] - dot(w_ref[rows, :3 * part], right)

    for h in range(HALVES):
        keep(col, h)
    weigh(col)
    take(near.at[sibling], sib_recv)
    for h in range(HALVES):
        keep(sibling, h)
    for i in range(chunks):
        c_copy(i).wait()
        near_job(chunk_of(*order[i]))
    arrive(0)
    arrive_sibling(0)
    produce(0)
    weigh(sibling)
    arrive(1)
    pass_on(0)
    arrive_sibling(1)
    produce(1)
    collect(0)
    pass_on(1)
    weigh(across)
    weigh(across_sibling)
    pair(0)
    collect(1)
    finish(0)
    pair(1)
    for e in group:
        spread(0, e)
    finish(1)
    for d in dims:
        update(chunk_of(d, 0))
    for e in range(RING):
        hand_on(0, e)
    for e in group:
        spread(1, e)
    near_gathered(0)
    hand_on(1, 0)
    for d in dims:
        update(chunk_of(d, 1))
    hand_on(1, 1)
    hand_on(1, 2)
    for d in dims:
        update(chunk_of(d, -1))
    hand_on(1, 3)
    far_gathered(0)
    for d in dims:
        update(chunk_of(d, 2))
    near_gathered(1)
    far_gathered(1)

    take(near.at[pl.ds(0, 3)], send)
    for h in range(HALVES):
        take(passing.at[h], send)
        take(got1.at[h], send)
        take(got2.at[h], send)
        take(got3.at[h], send)
        take(got2.at[h], send)
        take(res.at[pl.ds(0, 3)], send)


def update_kernel(c_ref, w_ref, res, out_hbm, stage, sem):
    chunks, height, width = c_ref.shape
    part = res.shape[1] // HALVES
    slots = stage.shape[0]
    pieces = 4
    size = height // pieces

    def out_copy(chunk, slot):
        return pltpu.make_async_copy(
            stage.at[slot], out_hbm.at[:, pl.ds(pl.multiple_of(chunk * width, width), width)], sem.at[slot]
        )

    def step(chunk, carry):
        slot = lax.rem(chunk, slots)

        @pl.when(chunk >= slots)
        def _():
            out_copy(chunk - slots, slot).wait()

        right = stacked(res[chunk, part:])
        for p in range(pieces):
            rows = slice(p * size, (p + 1) * size)
            stage[slot, rows] = c_ref[chunk, rows] - dot(w_ref[rows, 3 * part:], right)
        out_copy(chunk, slot).start()
        return carry

    lax.fori_loop(0, chunks, step, 0)
    for i in range(slots):
        chunk = chunks - slots + i
        out_copy(chunk, chunk % slots).wait()


def grid_shards(trailing, vectors, tfactor):
    height, columns = trailing.shape
    own, depth = vectors.shape
    chunks = 2 * RING
    width = columns // chunks
    blocks = height // own
    part = depth // HALVES
    sub = part // RING
    dma = pltpu.SemaphoreType.DMA
    vmem = pl.BlockSpec(memory_space=pltpu.VMEM)
    hbm = pl.BlockSpec(memory_space=pltpu.HBM)
    held, w_ref, res = pl.pallas_call(
        sum_kernel,
        out_shape=(
            pltpu.VMEM((chunks, height, width), F32),
            pltpu.VMEM((height, 3 * depth), BF16),
            pltpu.VMEM((chunks, depth, width), F32),
        ),
        in_specs=[hbm, hbm, hbm],
        out_specs=(vmem, vmem, vmem),
        scratch_shapes=[
            pltpu.VMEM((blocks, own, depth), F32),
            pltpu.VMEM((HALVES, chunks, part, width), F32),
            pltpu.VMEM((HALVES, blocks, 2 * part, own), BF16),
            pltpu.VMEM((HALVES, 2, 2, part // 2, width), F32),
            pltpu.VMEM((HALVES, 2, 2, part, width), F32),
            pltpu.VMEM((HALVES, 2, RING - 1, sub, width), F32),
            pltpu.VMEM((HALVES, 2, sub, width), F32),
            pltpu.VMEM((depth, depth), F32),
            dma((chunks,)), dma((2,)),
            dma, dma, dma((HALVES, V_PIECES)), dma((HALVES,)),
            dma((HALVES, 2, 2)), dma((HALVES, 2)), dma((HALVES, 2)), dma((HALVES, 2)),
            dma((HALVES, 2, RING)), dma((HALVES, 2, RING)), dma((HALVES,)), dma((HALVES,)),
        ],
        compiler_params=pltpu.CompilerParams(
            collective_id=0, has_side_effects=True, vmem_limit_bytes=42 << 20
        ),
    )(trailing, vectors, tfactor)
    slots = 4
    return pl.pallas_call(
        update_kernel,
        out_shape=jax.ShapeDtypeStruct((height, columns), F32),
        in_specs=[vmem, vmem, vmem],
        out_specs=hbm,
        scratch_shapes=[pltpu.VMEM((slots, height, width), F32), dma((slots,))],
        compiler_params=pltpu.CompilerParams(vmem_limit_bytes=20 << 20),
    )(held, w_ref, res)


def plain_shards(trailing, vectors, tfactor):
    dot = functools.partial(jnp.dot, precision=lax.Precision.HIGH, preferred_element_type=F32)
    near_vectors = lax.all_gather(vectors, "col", axis=0, tiled=True)
    summed = lax.psum(dot(near_vectors.T, trailing), "row")
    return trailing - dot(near_vectors, dot(tfactor, summed))


def solution(mesh):
    placed = (P("row", "col"), P(("row", "col"), None), P())
    fits = mesh.shape["row"] == 2 * RING * RING and mesh.shape["col"] == 4

    def shards(trailing, vectors, tfactor):
        if fits and trailing.shape == (2048, 2048) and vectors.shape == (512, 256):
            return grid_shards(trailing, vectors, tfactor)
        return plain_shards(trailing, vectors, tfactor)

    return jax.shard_map(
        shards, mesh=mesh, in_specs=placed, out_specs=P("row", "col"), check_vma=False
    )
```

time: 68.5 us -> 59.6 us (0.87)
  Pallas kernels: 66.3 us -> 59.5 us
  local copies, waits for them, and re-layouts: 1.99 us -> 0 us
    pallas_call x1, Pallas kernels: 57 us -> 52.4 us  [grid_shards(): pl.pallas_call(sum_kernel, out_shape=(pltpu.VMEM((chunks, height, width),...]
    pallas_call x1, Pallas kernels: 9.25 us -> 7.03 us  [grid_shards(): pl.pallas_call(update_kernel, out_shape=jax.ShapeDtypeStruct((height, col...]
    unnamed x4 -> x0, local copies, waits for them, and re-layouts: 1.99 us -> none
where the time goes in v2:
time: 59.6 us; the launch traced here: 59.5 us
  Pallas kernels  59.5 us (100%)
    pallas_call x1, Pallas kernels, grid_shards(): pl.pallas_call(sum_kernel, out_shape=(pltpu.VMEM((chunks, height, width),...  52.4 us
    pallas_call x1, Pallas kernels, grid_shards(): pl.pallas_call(update_kernel, out_shape=jax.ShapeDtypeStruct((height, col...  7.03 us

profile of v2, /device:TPU:0, one launch (start us, length us, event | category | flops | bytes accessed | tf_op | source)
XLA Modules:
  0.0 59.5 jit_solution(6987765255853128083)
XLA Ops:
  0.0 52.4 %shard_map.37 = (f32[8,2048,256]{2,1,0:T(8,128)S(1)}, bf16[2048,768]{1,0:T(8,128)(2,1)S(1)}, f32[8,256,256]{2,1,0:T(8,128)S(1)}) custom-call(f32[2048,2048]{1,0:T(8,128)} %c_hbm.1, f32[512,256]{1,0:T(8,128)} %v_hbm.1, f32[256,256]{1,0:T(8,128)} %t_hbm.1), custom_call_target="tpu_custom_call" | custom-call | tf_op jit(solution)/shard_map/pallas_call | solution.py:386
  52.4 7.0 %shard_map.38 = f32[2048,2048]{1,0:T(8,128)} custom-call(f32[8,2048,256]{2,1,0:T(8,128)S(1)} %get-tuple-element.8.c_ref, bf16[2048,768]{1,0:T(8,128)(2,1)S(1)} %get-tuple-element.9.w_ref, f32[8,256,256]{2,1,0:T(8,128)S(1)} %get-tuple-element.10.res), custom_call_target="tpu_custom_call" | custom-call | tf_op jit(solution)/shard_map/pallas_call | solution.py:414

commit v3 on v2

v3 whole, which is shorter than its diff:
```python
import functools

import jax
import jax.numpy as jnp
from jax import lax
from jax.experimental import pallas as pl
from jax.experimental.pallas import tpu as pltpu
from jax.sharding import PartitionSpec as P

MESH = pl.DeviceIdType.MESH
F32, BF16 = jnp.float32, jnp.bfloat16
RING = 4
HALF = 128
PARTS = ((0, 128), (128, 64), (192, 64))
DIRECT = (False, False, True)
V_PIECES = 2
WAYS = (1, -1)
OTHERS = (0, 1, -1, 2)


def split(x):
    high = x.astype(BF16)
    return high, (x - high.astype(F32)).astype(BF16)


def dot(a, b):
    return jnp.dot(a, b, preferred_element_type=F32)


def dot3(a_high, a_low, b_high, b_low):
    return dot(a_high, b_high) + (dot(a_low, b_high) + dot(a_high, b_low))


def stacked_halves(ref, chunk, first, count):
    rows = []
    for at in range(first, first + count, HALF):
        high, low = split(ref[chunk, at:at + HALF])
        rows += [high, high, low]
    return jnp.concatenate(rows, axis=0)


def sum_kernel(
    c_hbm, v_hbm, t_hbm, c_ref, w_ref, res,
    v_ref, near, acc, vt, vt_far, c_high, c_low, passing, got1, far1, got2, got3, t_ref, c_sem, l_sem,
    send, sib_recv, v_recv, f_recv, a_recv, r1_recv, r2_recv, y_recv, g2_recv, g1_recv, near_recv, far_recv,
):
    row, col = lax.axis_index("row"), lax.axis_index("col")
    core, y_hi = lax.rem(col, 2), lax.div(col, 2)
    z, x, y_lo = lax.div(row, 2 * RING), lax.rem(lax.div(row, 2), RING), lax.rem(row, 2)
    sibling = y_hi * 2 + (1 - core)
    across = (1 - y_hi) * 2 + core
    across_sibling = (1 - y_hi) * 2 + (1 - core)
    blocks, depth, own = near.shape
    chunks, height, width = c_ref.shape
    group = range(1, RING)
    dims = range(2)
    pos, other = (x, z), (z, x)

    def wrap(i):
        return lax.rem(i + RING, RING)

    def target(d, away, across_other, flip):
        first = wrap(pos[d] + away)
        second = wrap(other[d] + across_other)
        zz, xx = (second, first) if d == 0 else (first, second)
        return (zz * (2 * RING) + xx * 2 + lax.rem(y_lo + flip, 2), col)

    def remote(src, dst, recv, to):
        return pltpu.make_async_remote_copy(
            src_ref=src, dst_ref=dst, send_sem=send, recv_sem=recv, device_id=to, device_id_type=MESH
        )

    def take(ref, sem):
        pltpu.make_async_copy(ref, ref, sem).wait()

    def chunk_of(d, away):
        return d * RING + wrap(pos[d] + away)

    order = [(d, away) for away in (2, 1, -1, 0) for d in dims]

    def c_copy(i):
        chunk = chunk_of(*order[i])
        return pltpu.make_async_copy(
            c_hbm.at[:, pl.ds(pl.multiple_of(chunk * width, width), width)], c_ref.at[chunk], c_sem.at[i]
        )

    v_copy = pltpu.make_async_copy(v_hbm, v_ref, l_sem.at[0])
    t_copy = pltpu.make_async_copy(t_hbm, t_ref, l_sem.at[1])
    v_copy.start()
    t_copy.start()

    barrier = pltpu.get_barrier_semaphore()
    friends = [(row, sibling), (row, across)]
    friends += [target(d, away, 0, 0) for d in dims for away in (1, -1, 2)]
    friends += [target(0, 0, 0, 1)]
    for friend in friends:
        pl.semaphore_signal(barrier, inc=1, device_id=friend, device_id_type=MESH)
    v_copy.wait()
    t_copy.wait()
    for i in range(chunks):
        c_copy(i).start()
    pl.semaphore_wait(barrier, len(friends))

    def rows_in(h, share=1, place=0):
        first, count = PARTS[h]
        return pl.ds(pl.multiple_of(first // share + place * (count // share), 8), count // share)

    def v_copy_across(h, p):
        size = own // V_PIECES
        there = near.at[col, rows_in(h), pl.ds(p * size, size)]
        return remote(there, there, v_recv.at[h, p], (row, across))

    def forward(h, p):
        size = own // V_PIECES
        there = near.at[across, rows_in(h), pl.ds(p * size, size)]
        return remote(there, there, f_recv.at[h], (row, sibling))

    for h, (first, count) in enumerate(PARTS):
        for at in range(-(-first // HALF) * HALF, first + count, HALF):
            near[col, at:at + HALF] = v_ref[:, at:at + HALF].T
        for p in range(V_PIECES):
            v_copy_across(h, p).start()
    sib = remote(near.at[col], near.at[col], sib_recv, (row, sibling))
    sib.start()

    def keep(ref, block, first, count, lanes=slice(None)):
        high, low = split(near[block, first:first + count])
        ref[2 * first:2 * first + count, lanes] = high
        ref[2 * first + count:2 * (first + count), lanes] = low

    def arrive(h):
        for p in range(V_PIECES):
            v_copy_across(h, p).wait_recv()
            forward(h, p).start()
        keep(vt_far, across, *PARTS[h], slice(0, own))

    def arrive_sibling(h):
        take(near.at[across_sibling, rows_in(h)], f_recv.at[h])
        keep(vt_far, across_sibling, *PARTS[h], slice(own, 2 * own))

    def product(ref, first, count, high, low):
        both = dot(ref[2 * first:2 * (first + count)], high)
        return both[:count] + (both[count:] + dot(ref[2 * first:2 * first + count], low))

    def piece(away, block):
        rows = pl.ds(pl.multiple_of(block * own, own), own)
        return split(jnp.concatenate([c_ref[chunk_of(d, away), rows] for d in dims], axis=1))

    def near_job(away):
        c0, c1 = piece(away, col), piece(away, sibling)
        for first in range(0, depth, HALF):
            total = product(vt.at[0], first, HALF, *c0) + product(vt.at[1], first, HALF, *c1)
            for d in dims:
                acc[chunk_of(d, away), first:first + HALF] = total[:, d * width:(d + 1) * width]

    def prepare(away):
        for i, block in enumerate((across, across_sibling)):
            c_high[away, i * own:(i + 1) * own], c_low[away, i * own:(i + 1) * own] = piece(away, block)

    def job(away, h, which=slice(None)):
        first, count = PARTS[h]
        total = product(vt_far.at[:, which], first, count, c_high[away, which], c_low[away, which])
        for d in dims:
            acc[chunk_of(d, away), first:first + count] += total[:, d * width:(d + 1) * width]

    def weigh(block):
        t_high, t_low = split(t_ref[...].T)
        high, low = split(near[block])
        high, low = split(dot3(t_high, t_low, high, low).T)
        rows = pl.ds(pl.multiple_of(block * own, own), own)
        for first in range(0, depth, HALF):
            lanes = slice(first, first + HALF)
            w_ref[rows, 3 * first:3 * first + HALF] = high[:, lanes]
            w_ref[rows, 3 * first + HALF:3 * first + 2 * HALF] = low[:, lanes]
            w_ref[rows, 3 * first + 2 * HALF:3 * (first + HALF)] = high[:, lanes]

    def half_rows(h, way):
        first, count = PARTS[h]
        return pl.ds(first + way * (count // 2), count // 2)

    def upper(h, way):
        return half_rows(h, way)

    def lower(h, way):
        return half_rows(h, 1 - way)

    def a_copy(h, d, way):
        return remote(
            acc.at[chunk_of(d, 2), upper(h, way)], passing.at[d, way, rows_in(h, 2)],
            a_recv.at[h, d, way], target(d, WAYS[way], 0, 0),
        )

    def b_copy(h, d, way):
        rows = rows_in(h) if DIRECT[h] else lower(h, way)
        return remote(
            acc.at[chunk_of(d, WAYS[way]), rows], got1.at[d, way, rows], r1_recv.at[h, d], target(d, WAYS[way], 0, 0)
        )

    def s_copy(h, d, way):
        rows = upper(h, way)
        return remote(
            acc.at[chunk_of(d, WAYS[way]), rows], got1.at[d, way, rows], r1_recv.at[h, d], target(d, WAYS[way], 0, 0)
        )

    def far_copy(h, d):
        return remote(
            acc.at[chunk_of(d, 2), rows_in(h)], far1.at[d, rows_in(h)], a_recv.at[h, d, 0], target(d, 2, 0, 0)
        )

    def place_rows(h, d, away):
        first, count = PARTS[h]
        sub = count // RING
        return pl.ds(pl.multiple_of(first + wrap(other[d] + away) * sub, sub), sub)

    def r2_copy(h, d, e):
        return remote(
            acc.at[chunk_of(d, 0), place_rows(h, d, OTHERS[e])], got2.at[d, e - 1, rows_in(h, RING)], r2_recv.at[h, d],
            target(d, 0, OTHERS[e], 0),
        )

    def y_copy(h, d):
        return remote(
            acc.at[chunk_of(d, 0), place_rows(h, d, 0)], got3.at[d, rows_in(h, RING)], y_recv.at[h, d],
            target(d, 0, 0, 1),
        )

    def g2_copy(h, d, e):
        ref = res.at[chunk_of(d, 0), place_rows(h, d, 0)]
        return remote(ref, ref, g2_recv.at[h, d, e], target(d, 0, OTHERS[e], 0))

    def g1_copy(h, d, way, e):
        ref = res.at[chunk_of(d, 0), place_rows(h, d, -OTHERS[e])]
        recv = g1_recv.at[h, d, e] if way == e % 2 and not DIRECT[h] else near_recv.at[h]
        return remote(ref, ref, recv, target(d, WAYS[way], 0, 0))

    def gf_copy(h, d, e):
        way = e % 2
        chunk = chunk_of(d, 0) if DIRECT[h] else chunk_of(d, -WAYS[way])
        ref = res.at[chunk, place_rows(h, d, -OTHERS[e])]
        return remote(ref, ref, far_recv.at[h], target(d, 2 if DIRECT[h] else WAYS[way], 0, 0))

    def produce(h):
        job(2, h, slice(0, own))
        arrive_sibling(h)
        job(2, h, slice(own, 2 * own))
        for d in dims:
            if DIRECT[h]:
                far_copy(h, d).start()
            else:
                for way in range(2):
                    a_copy(h, d, way).start()
        for way in range(2):
            job(WAYS[way] % RING, h)
            for d in dims:
                b_copy(h, d, way).start()
        job(0, h)

    def pass_on(h):
        for d in dims:
            for way in range(2):
                a_copy(h, d, way).wait_recv()
                acc[chunk_of(d, WAYS[way]), upper(h, way)] += passing[d, way, rows_in(h, 2)]
                s_copy(h, d, way).start()

    def collect(h):
        rows = rows_in(h)
        for d in dims:
            take(got1.at[d, :, rows], r1_recv.at[h, d])
            total = got1[d, 0, rows] + got1[d, 1, rows]
            if DIRECT[h]:
                take(far1.at[d, rows], a_recv.at[h, d, 0])
                total += far1[d, rows]
            acc[chunk_of(d, 0), rows] += total
            for e in group:
                r2_copy(h, d, e).start()

    def pair(h):
        rows = rows_in(h, RING)
        for d in dims:
            take(got2.at[d, :, rows], r2_recv.at[h, d])
            acc[chunk_of(d, 0), place_rows(h, d, 0)] += got2[d, 0, rows] + (got2[d, 1, rows] + got2[d, 2, rows])
            y_copy(h, d).start()

    def send_on(h, d, e):
        if DIRECT[h]:
            gf_copy(h, d, e).start()
        for way in range(2):
            g1_copy(h, d, way, e).start()

    def finish(h):
        for d in dims:
            mine = chunk_of(d, 0)
            y_copy(h, d).wait_recv()
            res[mine, place_rows(h, d, 0)] = acc[mine, place_rows(h, d, 0)] + got3[d, rows_in(h, RING)]
            for e in group:
                g2_copy(h, d, e).start()
            send_on(h, d, 0)

    def spread(h):
        for e in group:
            for d in dims:
                g2_copy(h, d, e).wait_recv()
                send_on(h, d, e)

    def hand_on(h, e):
        for d in dims:
            g1_copy(h, d, e % 2, e).wait_recv()
            gf_copy(h, d, e).start()

    def near_gathered(h):
        take(got1.at[:, :, rows_in(h)] if DIRECT[h] else far1.at[:, rows_in(h)], near_recv.at[h])

    def far_gathered(h):
        take(far1.at[:, rows_in(h)], far_recv.at[h])

    def update(chunk, first, count):
        right = stacked_halves(res, chunk, first, count)
        for b in range(blocks):
            rows = slice(b * own, (b + 1) * own)
            c_ref[chunk, rows] = c_ref[chunk, rows] - dot(w_ref[rows, 3 * first:3 * (first + count)], right)

    for first in range(0, depth, HALF):
        keep(vt.at[0], col, first, HALF)
    weigh(col)
    take(near.at[sibling], sib_recv)
    for first in range(0, depth, HALF):
        keep(vt.at[1], sibling, first, HALF)
    for i in range(0, chunks, 2):
        c_copy(i).wait()
        c_copy(i + 1).wait()
        near_job(order[i][1])
    for away in range(RING):
        prepare((away + 2) % RING)
    arrive(0)
    produce(0)
    last = len(PARTS) - 1
    if last == 2:
        arrive(1)
        produce(1)
    arrive(last)
    pass_on(0)
    produce(last)
    if last == 2 and not DIRECT[1]:
        pass_on(1)
    collect(0)
    if not DIRECT[last]:
        pass_on(last)
    weigh(sibling)
    weigh(across)
    if last == 2:
        collect(1)
    weigh(across_sibling)
    collect(2)
    pair(0)
    pair(1)
    pair(2)
    finish(0)
    finish(1)
    finish(2)
    spread(0)
    spread(1)
    for d in dims:
        update(chunk_of(d, 0), 0, HALF)
    for e in range(RING):
        hand_on(0, e)
    spread(last)
    if last == 2 and not DIRECT[1]:
        for e in range(RING):
            hand_on(1, e)
    if not DIRECT[last]:
        hand_on(last, 0)
    for d in dims:
        update(chunk_of(d, 0), HALF, HALF)
    near_gathered(0)
    if not DIRECT[last]:
        for e in range(1, RING):
            hand_on(last, e)
    for away in WAYS:
        for d in dims:
            update(chunk_of(d, away), 0, HALF)
    far_gathered(0)
    for h in range(1, len(PARTS)):
        near_gathered(h)
        far_gathered(h)

    take(near.at[pl.ds(0, 3)], send)
    for h in range(len(PARTS)):
        if DIRECT[h]:
            take(far1.at[:, rows_in(h)], send)
            for way in range(2):
                take(far1.at[:, rows_in(h)], send)
        else:
            take(passing.at[:, :, rows_in(h, 2)], send)
            take(got1.at[:, :, rows_in(h)], send)
        take(got2.at[:, :, rows_in(h, RING)], send)
        take(got3.at[:, rows_in(h, RING)], send)
        take(got2.at[:, :, rows_in(h, RING)], send)
        take(got1.at[:, :, rows_in(h)], send)
        take(far1.at[:, rows_in(h)], send)


def update_kernel(c_ref, w_ref, res, out_hbm, stage, sem):
    row = lax.axis_index("row")
    places = lax.rem(lax.div(row, 2), RING), lax.div(row, 2 * RING)
    chunks, height, width = c_ref.shape
    depth = res.shape[1]
    slots = stage.shape[0]
    pieces = 4
    size = height // pieces

    def chunk_of(i):
        d, away = lax.rem(i, 2), lax.div(i, 2)
        return d * RING + lax.rem(jnp.where(d == 0, places[0], places[1]) + jnp.where(away == 2, 3, jnp.where(away == 3, 2, away)), RING)

    def out_copy(i, ref, slot):
        lanes = pl.ds(pl.multiple_of(chunk_of(i) * width, width), width)
        return pltpu.make_async_copy(ref, out_hbm.at[:, lanes], sem.at[slot])

    for i in range(2):
        out_copy(i, c_ref.at[chunk_of(i)], slots + i).start()

    def step(i, carry, first):
        slot = lax.rem(i, slots)

        @pl.when(i >= slots + 2)
        def _():
            out_copy(i - slots, stage.at[slot], slot).wait()

        right = stacked_halves(res, chunk_of(i), first, depth - first)
        for p in range(pieces):
            rows = slice(p * size, (p + 1) * size)
            stage[slot, rows] = c_ref[chunk_of(i), rows] - dot(w_ref[rows, 3 * first:], right)
        out_copy(i, stage.at[slot], slot).start()
        return carry

    lax.fori_loop(2, 6, functools.partial(step, first=HALF), 0)
    lax.fori_loop(6, chunks, functools.partial(step, first=0), 0)
    for i in range(2):
        out_copy(i, c_ref.at[chunk_of(i)], slots + i).wait()
    for i in range(max(2, chunks - slots), chunks):
        out_copy(i, stage.at[i % slots], i % slots).wait()


def grid_shards(trailing, vectors, tfactor):
    height, columns = trailing.shape
    own, depth = vectors.shape
    chunks = 2 * RING
    width = columns // chunks
    blocks = height // own
    parts = len(PARTS)
    dma = pltpu.SemaphoreType.DMA
    vmem = pl.BlockSpec(memory_space=pltpu.VMEM)
    hbm = pl.BlockSpec(memory_space=pltpu.HBM)
    held, w_ref, res = pl.pallas_call(
        sum_kernel,
        out_shape=(
            pltpu.VMEM((chunks, height, width), F32),
            pltpu.VMEM((height, 3 * depth), BF16),
            pltpu.VMEM((chunks, depth, width), F32),
        ),
        in_specs=[hbm, hbm, hbm],
        out_specs=(vmem, vmem, vmem),
        scratch_shapes=[
            pltpu.VMEM((own, depth), F32),
            pltpu.VMEM((blocks, depth, own), F32),
            pltpu.VMEM((chunks, depth, width), F32),
            pltpu.VMEM((2, 2 * depth, own), BF16),
            pltpu.VMEM((2 * depth, 2 * own), BF16),
            pltpu.VMEM((RING, 2 * own, 2 * width), BF16),
            pltpu.VMEM((RING, 2 * own, 2 * width), BF16),
            pltpu.VMEM((2, 2, depth // 2, width), F32),
            pltpu.VMEM((2, 2, depth, width), F32),
            pltpu.VMEM((2, depth, width), F32),
            pltpu.VMEM((2, RING - 1, depth // RING, width), F32),
            pltpu.VMEM((2, depth // RING, width), F32),
            pltpu.VMEM((depth, depth), F32),
            dma((chunks,)), dma((2,)),
            dma, dma, dma((parts, V_PIECES)), dma((parts,)),
            dma((parts, 2, 2)), dma((parts, 2)), dma((parts, 2)), dma((parts, 2)),
            dma((parts, 2, RING)), dma((parts, 2, RING)), dma((parts,)), dma((parts,)),
        ],
        compiler_params=pltpu.CompilerParams(
            collective_id=0, has_side_effects=True, vmem_limit_bytes=42 << 20
        ),
    )(trailing, vectors, tfactor)
    slots = 4
    return pl.pallas_call(
        update_kernel,
        out_shape=jax.ShapeDtypeStruct((height, columns), F32),
        in_specs=[vmem, vmem, vmem],
        out_specs=hbm,
        scratch_shapes=[pltpu.VMEM((slots, height, width), F32), dma((slots + 2,))],
        compiler_params=pltpu.CompilerParams(vmem_limit_bytes=20 << 20),
    )(held, w_ref, res)


def plain_shards(trailing, vectors, tfactor):
    dot = functools.partial(jnp.dot, precision=lax.Precision.HIGH, preferred_element_type=F32)
    near_vectors = lax.all_gather(vectors, "col", axis=0, tiled=True)
    summed = lax.psum(dot(near_vectors.T, trailing), "row")
    return trailing - dot(near_vectors, dot(tfactor, summed))


def solution(mesh):
    placed = (P("row", "col"), P(("row", "col"), None), P())
    fits = mesh.shape["row"] == 2 * RING * RING and mesh.shape["col"] == 4

    def shards(trailing, vectors, tfactor):
        if fits and trailing.shape == (2048, 2048) and vectors.shape == (512, 256):
            return grid_shards(trailing, vectors, tfactor)
        return plain_shards(trailing, vectors, tfactor)

    return jax.shard_map(
        shards, mesh=mesh, in_specs=placed, out_specs=P("row", "col"), check_vma=False
    )
```

time: 59.6 us -> 56.7 us (0.951)
  Pallas kernels: 59.5 us -> 56.4 us
    pallas_call x1, Pallas kernels: 52.4 us -> 50.2 us  [grid_shards(): pl.pallas_call(sum_kernel, out_shape=(pltpu.VMEM((chunks, height, width),...]
    pallas_call x1, Pallas kernels: 7.03 us -> 6.23 us  [grid_shards(): pl.pallas_call(update_kernel, out_shape=jax.ShapeDtypeStruct((height, col...]
where the time goes in v3:
time: 56.7 us; the launch traced here: 56.6 us
  Pallas kernels  56.4 us (99%)
    pallas_call x1, Pallas kernels, grid_shards(): pl.pallas_call(sum_kernel, out_shape=(pltpu.VMEM((chunks, height, width),...  50.2 us
    pallas_call x1, Pallas kernels, grid_shards(): pl.pallas_call(update_kernel, out_shape=jax.ShapeDtypeStruct((height, col...  6.23 us

profile of v3, /device:TPU:0, one launch (start us, length us, event | category | flops | bytes accessed | tf_op | source)
XLA Modules:
  0.0 56.6 jit_solution(12474035018596698768)
XLA Ops:
  0.0 50.2 %shard_map.37 = (f32[8,2048,256]{2,1,0:T(8,128)S(1)}, bf16[2048,768]{1,0:T(8,128)(2,1)S(1)}, f32[8,256,256]{2,1,0:T(8,128)S(1)}) custom-call(f32[2048,2048]{1,0:T(8,128)} %c_hbm.1, f32[512,256]{1,0:T(8,128)} %v_hbm.1, f32[256,256]{1,0:T(8,128)} %t_hbm.1), custom_call_target="tpu_custom_call" | custom-call | tf_op jit(solution)/shard_map/pallas_call | solution.py:454
  50.2 6.2 %shard_map.38 = f32[2048,2048]{1,0:T(8,128)} custom-call(f32[8,2048,256]{2,1,0:T(8,128)S(1)} %get-tuple-element.8.c_ref, bf16[2048,768]{1,0:T(8,128)(2,1)S(1)} %get-tuple-element.9.w_ref, f32[8,256,256]{2,1,0:T(8,128)S(1)} %get-tuple-element.10.res), custom_call_target="tpu_custom_call" | custom-call | tf_op jit(solution)/shard_map/pallas_call | solution.py:487

commit v4 on v3

--- a/solution.py
+++ b/solution.py
@@ -342,14 +342,13 @@
     produce(last)
     if last == 2 and not DIRECT[1]:
         pass_on(1)
+    weigh(sibling)
+    weigh(across)
     collect(0)
     if not DIRECT[last]:
         pass_on(last)
-    weigh(sibling)
-    weigh(across)
-    if last == 2:
-        collect(1)
     weigh(across_sibling)
+    collect(1)
     collect(2)
     pair(0)
     pair(1)

time: 56.7 us -> 55.4 us (0.977)
  Pallas kernels: 56.4 us -> 55.2 us
    pallas_call x1, Pallas kernels: 50.2 us -> 48.9 us  [grid_shards(): pl.pallas_call(sum_kernel, out_shape=(pltpu.VMEM((chunks, height, width),...]
where the time goes in v4:
time: 55.4 us; the launch traced here: 55.3 us
  Pallas kernels  55.2 us (100%)
    pallas_call x1, Pallas kernels, grid_shards(): pl.pallas_call(sum_kernel, out_shape=(pltpu.VMEM((chunks, height, width),...  48.9 us
    pallas_call x1, Pallas kernels, grid_shards(): pl.pallas_call(update_kernel, out_shape=jax.ShapeDtypeStruct((height, col...  6.23 us

profile of v4, /device:TPU:0, one launch (start us, length us, event | category | flops | bytes accessed | tf_op | source)
XLA Modules:
  0.0 55.3 jit_solution(11910308001869162131)
XLA Ops:
  0.0 48.9 %shard_map.37 = (f32[8,2048,256]{2,1,0:T(8,128)S(1)}, bf16[2048,768]{1,0:T(8,128)(2,1)S(1)}, f32[8,256,256]{2,1,0:T(8,128)S(1)}) custom-call(f32[2048,2048]{1,0:T(8,128)} %c_hbm.1, f32[512,256]{1,0:T(8,128)} %v_hbm.1, f32[256,256]{1,0:T(8,128)} %t_hbm.1), custom_call_target="tpu_custom_call" | custom-call | tf_op jit(solution)/shard_map/pallas_call | solution.py:453
  48.9 6.2 %shard_map.38 = f32[2048,2048]{1,0:T(8,128)} custom-call(f32[8,2048,256]{2,1,0:T(8,128)S(1)} %get-tuple-element.8.c_ref, bf16[2048,768]{1,0:T(8,128)(2,1)S(1)} %get-tuple-element.9.w_ref, f32[8,256,256]{2,1,0:T(8,128)S(1)} %get-tuple-element.10.res), custom_call_target="tpu_custom_call" | custom-call | tf_op jit(solution)/shard_map/pallas_call | solution.py:486

commit v5 on v4

--- a/solution.py
+++ b/solution.py
@@ -348,8 +348,8 @@
     if not DIRECT[last]:
         pass_on(last)
     weigh(across_sibling)
+    collect(2)
     collect(1)
-    collect(2)
     pair(0)
     pair(1)
     pair(2)

time: 55.4 us -> 55.4 us (level)
  no operation moved by 1% of the time
where the time goes in v5:
time: 55.4 us; the launch traced here: 55.3 us
  Pallas kernels  55.1 us (99%)
    pallas_call x1, Pallas kernels, grid_shards(): pl.pallas_call(sum_kernel, out_shape=(pltpu.VMEM((chunks, height, width),...  48.9 us
    pallas_call x1, Pallas kernels, grid_shards(): pl.pallas_call(update_kernel, out_shape=jax.ShapeDtypeStruct((height, col...  6.23 us

profile of v5, /device:TPU:0, one launch (start us, length us, event | category | flops | bytes accessed | tf_op | source)
XLA Modules:
  0.0 55.3 jit_solution(2131402464513891085)
XLA Ops:
  0.0 48.9 %shard_map.37 = (f32[8,2048,256]{2,1,0:T(8,128)S(1)}, bf16[2048,768]{1,0:T(8,128)(2,1)S(1)}, f32[8,256,256]{2,1,0:T(8,128)S(1)}) custom-call(f32[2048,2048]{1,0:T(8,128)} %c_hbm.1, f32[512,256]{1,0:T(8,128)} %v_hbm.1, f32[256,256]{1,0:T(8,128)} %t_hbm.1), custom_call_target="tpu_custom_call" | custom-call | tf_op jit(solution)/shard_map/pallas_call | solution.py:453
  48.9 6.2 %shard_map.38 = f32[2048,2048]{1,0:T(8,128)} custom-call(f32[8,2048,256]{2,1,0:T(8,128)S(1)} %get-tuple-element.8.c_ref, bf16[2048,768]{1,0:T(8,128)(2,1)S(1)} %get-tuple-element.9.w_ref, f32[8,256,256]{2,1,0:T(8,128)S(1)} %get-tuple-element.10.res), custom_call_target="tpu_custom_call" | custom-call | tf_op jit(solution)/shard_map/pallas_call | solution.py:486
